TPU v7x, 32 devices: a whole 2x2x4 slice. The times are simulated.
32 devices in a mesh: gx: 4 (over z), gy: 2 (over y), gz: 4 (over x, core).
Axes of the slice: x: 2, y: 2, z: 4, core: 2. Of those that a mesh axis runs over, the one named last changes fastest.
Arguments:
- iterate: float32 [32, 32, 512], P('gx', 'gy', 'gz'), may hold values from -6 to 6
- source: float32 [32, 32, 512], P('gx', 'gy', 'gz'), may hold values from -6 to 6
- reaction: float32 [32, 32, 512], P('gx', 'gy', 'gz'), may hold values from 0.05 to 1
- trial_powers: int32 [4], replicated, may hold values from 0 to 5
Outputs:
- newton_dir: float32 [32, 32, 512], P('gx', 'gy', 'gz')
- remnant: float32 [32, 32, 512], P('gx', 'gy', 'gz')
- layer_energies: float32 [4, 32], P(None, 'gx')
- energies: float32 [4], replicated
Inputs may be any that keep to these rules, and one draw needn't show every extreme that they name: `trial_powers`: trial k takes the step length 2 to the power minus entry k.
All inputs are finite; a program needn't handle non-finite values.
Results may differ from a plain program's by a relative error of at most 0.0003.
Values sent between devices are 32-bit elements; how exact they have to be, the bound alone decides.
A program may use at most 128 MiB of HBM per device.

v0:
```python
import jax
import jax.numpy as jnp
from jax import lax
from jax.sharding import PartitionSpec as P

ITERS = 4
LEVELS = 4
TRIALS = 4


cheb_mid = 1.15
cheb_half = 0.85


def padded_2(x, sides, width):
    for axis, dim in sides:
        size, length = (lax.axis_size(axis), x.shape[dim])
        up = [(i, (i + 1) % size) for i in range(size - 1)]
        down = [(j, i) for i, j in up]
        last = lax.slice_in_dim(x, length - width, length, axis=dim)
        first = lax.slice_in_dim(x, 0, width, axis=dim)
        before = lax.ppermute(last, axis, up)
        after = lax.ppermute(first, axis, down)
        x = jnp.concatenate([before, x, after], axis=dim)
    return x


def trim_rim(values, depth_cut):
    return values[depth_cut:-depth_cut, depth_cut:-depth_cut, depth_cut:-depth_cut]


def differences(padded):
    along_x = padded[1:, 1:-1, 1:-1] - padded[:-1, 1:-1, 1:-1]
    along_y = padded[1:-1, 1:, 1:-1] - padded[1:-1, :-1, 1:-1]
    along_z = padded[1:-1, 1:-1, 1:] - padded[1:-1, 1:-1, :-1]
    return (along_x, along_y, along_z)


def stiffness(gradient):
    square = gradient * gradient
    return (1.0 + 2.0 * square) / jnp.sqrt(1.0 + square)


def fluxes(gradient):
    return gradient * jnp.sqrt(1.0 + gradient * gradient)


def face_energy(gradient):
    square = 1.0 + gradient * gradient
    return (square * jnp.sqrt(square) - 1.0) / 3.0


def divergence(face_flows):
    return (
        face_flows[0][1:]
        - face_flows[0][:-1]
        + (face_flows[1][:, 1:] - face_flows[1][:, :-1])
        + (face_flows[2][:, :, 1:] - face_flows[2][:, :, :-1])
    )


def apply_operator(padded, weights, reaction):
    centre = padded[1:-1, 1:-1, 1:-1]
    gradient = differences(padded)
    face_flows = tuple((w * s for w, s in zip(weights, gradient)))
    return reaction * centre - divergence(face_flows)


def diagonal_of(weights, reaction):
    weight_x, weight_y, weight_z = weights
    return (
        reaction
        + weight_x[1:]
        + weight_x[:-1]
        + weight_y[:, 1:]
        + weight_y[:, :-1]
        + weight_z[:, :, 1:]
        + weight_z[:, :, :-1]
    )


def smooth(remnant, inverse, degree, operate):
    cheb_sigma = cheb_mid / cheb_half
    cheb_rho = 1.0 / cheb_sigma
    update = inverse * remnant / cheb_mid
    summed = update
    for sweep_idx in range(1, degree):
        remnant = remnant - operate(update)
        cheb_next = 1.0 / (2.0 * cheb_sigma - cheb_rho)
        update = cheb_next * cheb_rho * update + 2.0 * cheb_next / cheb_half * inverse * remnant
        summed = summed + update
        cheb_rho = cheb_next
    return (summed, remnant, update)


def pair_sum(values, axis_pos):
    old_shape = values.shape
    new_shape = old_shape[:axis_pos] + (old_shape[axis_pos] // 2, 2) + old_shape[axis_pos + 1 :]
    return jnp.sum(values.reshape(new_shape), axis=axis_pos + 1)


def restrict(values):
    return pair_sum(pair_sum(pair_sum(values, 0), 1), 2)


def prolong(values):
    return jnp.repeat(jnp.repeat(jnp.repeat(values, 2, 0), 2, 1), 2, 2)


def coarsen(weights, reaction):
    weight_x, weight_y, weight_z = weights
    coarse_x = pair_sum(pair_sum(weight_x[::2], 1), 2)
    coarse_y = pair_sum(pair_sum(weight_y[:, ::2], 0), 2)
    coarse_z = pair_sum(pair_sum(weight_z[:, :, ::2], 0), 1)
    return ((coarse_x, coarse_y, coarse_z), restrict(reaction))


def build_levels(weights, reaction):
    levels = [(weights, reaction, 1.0 / diagonal_of(weights, reaction))]
    for level_idx in range(1, LEVELS):
        weights, reaction = coarsen(weights, reaction)
        levels.append((weights, reaction, 1.0 / diagonal_of(weights, reaction)))
    return levels


def halo_one(values):
    return padded_2(values, (("gx", 0), ("gy", 1), ("gz", 2)), 1)


def precond_dot(left, right):
    return lax.psum(jnp.sum(left * right), ("gx", "gy", "gz"))


def curve_dot(left, right):
    return lax.psum(jnp.sum(left * right), ("gx", "gy", "gz"))


def vcycle(levels, level_depth, remnant, presmooth):
    weights, reaction, inverse = levels[level_depth]

    def operate(values):
        return apply_operator(halo_one(values), weights, reaction)

    if level_depth == len(levels) - 1:
        summed, _, _ = smooth(remnant, inverse, 3, operate)
        return summed
    summed, remnant, update = smooth(remnant, inverse, 2, operate)
    remnant = remnant - operate(update)
    correction = prolong(vcycle(levels, level_depth + 1, restrict(remnant), presmooth))
    summed = summed + correction
    remnant = remnant - operate(correction)
    smoothed, _, _ = smooth(remnant, inverse, 2, operate)
    return summed + smoothed


def on_device(iterate, source, reaction, trial_powers):
    size_x, size_y, size_z = iterate.shape
    counts = (lax.axis_size("gx"), lax.axis_size("gy"), lax.axis_size("gz"))
    padded = padded_2(iterate, (("gx", 0), ("gy", 1), ("gz", 2)), 1)
    gradient = differences(padded)
    weights = tuple((stiffness(s) for s in gradient))
    remnant = source - reaction * iterate + divergence(tuple((fluxes(s) for s in gradient)))
    levels = build_levels(weights, reaction)
    newton_dir = jnp.zeros_like(iterate)
    precond_out = vcycle(levels, 0, remnant, None)
    direction = precond_out
    precond_norm = precond_dot(remnant, precond_out)
    for iter_idx in range(ITERS):
        image_dir = apply_operator(halo_one(direction), weights, reaction)
        step_length = precond_norm / curve_dot(direction, image_dir)
        newton_dir = newton_dir + step_length * direction
        remnant = remnant - step_length * image_dir
        if iter_idx + 1 < ITERS:
            precond_out = vcycle(levels, 0, remnant, None)
            norm_next = precond_dot(remnant, precond_out)
            direction = precond_out + norm_next / precond_norm * direction
            precond_norm = norm_next
    dir_rim = padded_2(newton_dir, (("gx", 0), ("gy", 1), ("gz", 2)), 1)
    last_x = lax.axis_index("gx") == counts[0] - 1
    first_y = lax.axis_index("gy") == 0
    first_z = lax.axis_index("gz") == 0
    layer_rows = []
    for trial_idx in range(TRIALS):
        step_scale = jnp.exp2(-trial_powers[trial_idx].astype(jnp.float32))
        trial_field = padded + step_scale * dir_rim
        trial_slopes = differences(trial_field)
        energy_x = face_energy(trial_slopes[0])
        energy_y = face_energy(trial_slopes[1])
        energy_z = face_energy(trial_slopes[2])
        layer_sum = jnp.sum(energy_x[:-1], axis=(1, 2))
        layer_sum = layer_sum.at[-1].add(jnp.where(last_x, jnp.sum(energy_x[-1]), 0.0))
        layer_sum = (
            layer_sum
            + jnp.sum(energy_y[:, 1:], axis=(1, 2))
            + jnp.where(first_y, jnp.sum(energy_y[:, :1], axis=(1, 2)), 0.0)
        )
        layer_sum = (
            layer_sum
            + jnp.sum(energy_z[:, :, 1:], axis=(1, 2))
            + jnp.where(first_z, jnp.sum(energy_z[:, :, :1], axis=(1, 2)), 0.0)
        )
        inner_field = trim_rim(trial_field, 1)
        layer_sum = layer_sum + jnp.sum(
            0.5 * reaction * inner_field * inner_field - source * inner_field, axis=(1, 2)
        )
        layer_rows.append(layer_sum)
    layer_totals = lax.psum(jnp.stack(layer_rows), ("gy", "gz"))
    layer_cells = size_y * counts[1] * size_z * counts[2]
    layer_energies = layer_totals / layer_cells
    energy_totals = lax.psum(jnp.sum(layer_energies, axis=1), "gx")
    energies = energy_totals / (size_x * counts[0])
    return (newton_dir, remnant, layer_energies, energies)


def solution(mesh):
    placed = (P("gx", "gy", "gz"), P("gx", "gy", "gz"), P("gx", "gy", "gz"), P())
    return jax.shard_map(
        on_device,
        mesh=mesh,
        in_specs=placed,
        out_specs=(P("gx", "gy", "gz"), P("gx", "gy", "gz"), P(None, "gx"), P()),
        check_vma=False,
    )
```

profile of v0, /device:TPU:0, one launch (start us, length us, event | category | flops | bytes accessed | tf_op | source)
XLA Modules:
  0.0 1830.9 jit_solution(12728474767201894418)
XLA Ops:
  1.4 4.9 collective-permute-start.1
  100.6 4.9 collective-permute-start.25
  126.9 4.8 collective-permute-start.31
  289.0 4.9 collective-permute-start.73
  315.5 4.9 collective-permute-start.79
  382.9 44.5 %all-reduce = (f32[]{:T(128)}, f32[]{:T(128)}) all-reduce(f32[]{:T(128)} %get-tuple-element.61, f32[]{:T(128)} %get-tuple-element.60), channel_id=1, replica_groups=mesh['gx'=4,'gy'=2,'gz'=4] {'gx','gy','gz'}, use_global_device_ids=true, to_apply=%region_41.0 | all-reduce | flops 2 | bytes 16 | tf_op jit(solution)/shard_map/psum | solution.py:131
  502.2 4.9 collective-permute-start.115
  551.3 5.2 collective-permute-start.127
  690.6 4.9 collective-permute-start.163
  717.0 4.9 collective-permute-start.169
  761.5 44.5 %psum.72 = f32[]{:T(128)} all-reduce(f32[]{:T(128)} %get-tuple-element.120), channel_id=1, replica_groups=mesh['gx'=4,'gy'=2,'gz'=4] {'gx','gy','gz'}, use_global_device_ids=true, to_apply=%region_54.0 | all-reduce | flops 1 | bytes 8 | tf_op jit(solution)/shard_map/psum | solution.py:131
  829.7 44.5 %psum.73 = f32[]{:T(128)} all-reduce(f32[]{:T(128)} %get-tuple-element.118), channel_id=1, replica_groups=mesh['gx'=4,'gy'=2,'gz'=4] {'gx','gy','gz'}, use_global_device_ids=true, to_apply=%region_56.0 | all-reduce | flops 1 | bytes 8 | tf_op jit(solution)/shard_map/psum | solution.py:135
  948.4 4.9 collective-permute-start.205
  1136.3 4.9 collective-permute-start.253
  1162.7 4.9 collective-permute-start.259
  1207.2 44.5 %psum.74 = f32[]{:T(128)} all-reduce(f32[]{:T(128)} %get-tuple-element.94), channel_id=1, replica_groups=mesh['gx'=4,'gy'=2,'gz'=4] {'gx','gy','gz'}, use_global_device_ids=true, to_apply=%region_67.0 | all-reduce | flops 1 | bytes 8 | tf_op jit(solution)/shard_map/psum | solution.py:131
  1275.4 44.7 %psum.75 = f32[]{:T(128)} all-reduce(f32[]{:T(128)} %get-tuple-element.92), channel_id=1, replica_groups=mesh['gx'=4,'gy'=2,'gz'=4] {'gx','gy','gz'}, use_global_device_ids=true, to_apply=%region_69.0 | all-reduce | flops 1 | bytes 8 | tf_op jit(solution)/shard_map/psum | solution.py:135
  1394.3 4.9 collective-permute-start.295
  1582.6 4.9 collective-permute-start.343
  1609.1 4.9 collective-permute-start.349
  1653.7 44.5 %psum.76 = f32[]{:T(128)} all-reduce(f32[]{:T(128)} %get-tuple-element.68), channel_id=1, replica_groups=mesh['gx'=4,'gy'=2,'gz'=4] {'gx','gy','gz'}, use_global_device_ids=true, to_apply=%region_80.0 | all-reduce | flops 1 | bytes 8 | tf_op jit(solution)/shard_map/psum | solution.py:131
  1721.9 44.5 %psum.77 = f32[]{:T(128)} all-reduce(f32[]{:T(128)} %get-tuple-element.66), channel_id=1, replica_groups=mesh['gx'=4,'gy'=2,'gz'=4] {'gx','gy','gz'}, use_global_device_ids=true, to_apply=%region_82.83 | all-reduce | flops 1 | bytes 8 | tf_op jit(solution)/shard_map/psum | solution.py:135
  1802.4 14.6 psum.78
  1817.7 12.3 psum.79
  (1753 shorter events, 1395.4 us)
Async XLA Ops:
  109.1 9.1 collective-permute-start.27
  270.4 9.2 collective-permute-start.68
  271.6 9.8 collective-permute-start.69
  296.3 9.3 collective-permute-start.74
  297.6 9.8 collective-permute-start.75
  509.4 8.9 collective-permute-start.116
  510.7 9.1 collective-permute-start.117
  671.9 9.2 collective-permute-start.158
  673.2 9.8 collective-permute-start.159
  697.9 9.3 collective-permute-start.164
  699.2 9.8 collective-permute-start.165
  955.6 8.9 collective-permute-start.206
  956.8 9.1 collective-permute-start.207
  1117.6 9.2 collective-permute-start.248
  1118.9 9.8 collective-permute-start.249
  1143.6 9.3 collective-permute-start.254
  1144.9 9.8 collective-permute-start.255
  1401.5 8.9 collective-permute-start.296
  1402.8 9.4 collective-permute-start.297
  1563.9 9.2 collective-permute-start.338
  1565.2 9.8 collective-permute-start.339
  1589.9 9.3 collective-permute-start.344
  1591.2 9.8 collective-permute-start.345
  1775.1 9.2 collective-permute-start.369
  (359 other events, 2034.7 us)
where the time goes:
time: 1850 us; the launch traced here: 1830 us
  starting transfers between devices  977 us (53%)
  waiting for transfers between devices  400 us (22%)
  blocking collectives  339 us (18%)
  local copies, waits for them, and re-layouts  50.2 us (3%)
  other arithmetic  42.2 us (2%)
  between operations  23.4 us (1%)
    ppermute x186, starting transfers between devices, padded_2(): before = lax.ppermute(last, axis, up)  736 us
    ppermute x186, starting transfers between devices, padded_2(): after = lax.ppermute(first, axis, down)  240 us
    ppermute x186, waiting for transfers between devices, padded_2(): after = lax.ppermute(first, axis, down)  230 us
    psum x4, blocking collectives, precond_dot(): return lax.psum(jnp.sum(left * right), ('gx', 'gy', 'gz'))  178 us
    ppermute x186, waiting for transfers between devices, padded_2(): before = lax.ppermute(last, axis, up)  170 us
    psum x3, blocking collectives, curve_dot(): return lax.psum(jnp.sum(left * right), ('gx', 'gy', 'gz'))  134 us
  transfers between devices with their start and end apart: 372, of which 217 were waited for; matrix products, arithmetic and copies ran while one was open for 1% of the time, Pallas kernels for 0%

commit v1 on v0

v1 whole, which is shorter than its diff:
```python
import functools

import jax
import jax.numpy as jnp
from jax import lax
from jax.experimental import pallas as pl
from jax.experimental.pallas import tpu as pltpu
from jax.sharding import PartitionSpec as P

ITERS = 4
LEVELS = 4
TRIALS = 4
MID = 1.15
HALF = 0.85
SIGMA = MID / HALF
RHO0 = 1.0 / SIGMA
RHO1 = 1.0 / (2.0 * SIGMA - RHO0)
RHO2 = 1.0 / (2.0 * SIGMA - RHO1)
ROUND = 3
KEPT = ROUND
DG, INV, XM, XP, YM, YP, ZM, ZP, YB, ZB = range(10)
MESH = pl.DeviceIdType.MESH


def kernel(
    sizes, counts, tp_ref, it_ref, src_ref, rea_ref, dir_ref, rem_ref, le_ref, en_ref,
    sx, rx, sy, ry, sz, rz, ssem, rsem, lev0, lev1, lev2, lev3, p_ref, q_ref,
    phx, phy, phz, dhx, dhy, dhz, dot_pl, dot_x, en_pl, en_x, red_ssem, red_rsem,
):
    X, Y, Z = sizes
    nx, ny, nz = counts
    planes = ny * nz
    levs = (lev0, lev1, lev2, lev3)
    ix, iy, iz = lax.axis_index("gx"), lax.axis_index("gy"), lax.axis_index("gz")
    has = (ix > 0, ix < nx - 1, iy > 0, iy < ny - 1, iz > 0, iz < nz - 1)
    devs = (
        (ix - 1, iy, iz), (ix + 1, iy, iz), (ix, iy - 1, iz),
        (ix, iy + 1, iz), (ix, iy, iz - 1), (ix, iy, iz + 1),
    )
    send = (sx, sx, sy, sy, sz, sz)
    recv = (rx, rx, ry, ry, rz, rz)
    lane_y = lax.broadcasted_iota(jnp.int32, (Y, Z), 1)
    lane_1 = lax.broadcasted_iota(jnp.int32, (1, Z), 1)

    def rows_of(x):
        return lax.rem(lax.broadcasted_iota(jnp.int32, (x * Y, Z), 0), Y)

    def lanes_of(x):
        return lax.broadcasted_iota(jnp.int32, (x * Y, Z), 1)

    def cat(parts):
        return parts[0] if len(parts) == 1 else jnp.concatenate(parts, axis=0)

    def roll(v, shift, axis):
        return pltpu.roll(v, shift % v.shape[axis], axis)

    for d in range(6):
        @pl.when(jnp.logical_not(has[d]))
        def _():
            recv[d][:, d % 2] = jnp.zeros(recv[d].shape[:1] + recv[d].shape[2:], jnp.float32)

    def outgoing(d, slot):
        side = d % 2
        return pltpu.make_async_remote_copy(
            src_ref=send[d].at[slot, side],
            dst_ref=recv[d].at[slot, 1 - side],
            send_sem=ssem.at[slot, d],
            recv_sem=rsem.at[slot, d + 1 - 2 * side],
            device_id=devs[d],
            device_id_type=MESH,
        )

    def incoming(d, slot):
        side = d % 2
        return pltpu.make_async_remote_copy(
            src_ref=send[d].at[slot, side],
            dst_ref=recv[d].at[slot, side],
            send_sem=ssem.at[slot, d],
            recv_sem=rsem.at[slot, d],
            device_id=devs[d],
            device_id_type=MESH,
        )

    def go(d, slot):
        @pl.when(has[d])
        def _():
            outgoing(d, slot).start()

    def start(v, slot):
        x = v.shape[0] // Y
        sx[slot, 0] = v[:Y]
        sx[slot, 1] = v[-Y:]
        go(0, slot)
        go(1, slot)
        for i in range(x):
            sy[slot, 0, i : i + 1] = v[i * Y : i * Y + 1]
            sy[slot, 1, i : i + 1] = v[i * Y + Y - 1 : i * Y + Y]
        go(2, slot)
        go(3, slot)
        for side, lane in ((0, 0), (1, Z - 1)):
            packed = jnp.broadcast_to(v[:Y, lane : lane + 1], (Y, Z))
            for i in range(1, x):
                part = jnp.broadcast_to(v[i * Y : i * Y + Y, lane : lane + 1], (Y, Z))
                packed = jnp.where(lane_y == i, part, packed)
            sz[slot, side] = packed
        go(4, slot)
        go(5, slot)

    def finish(slot):
        for d in range(6):
            @pl.when(has[d])
            def _():
                copy = incoming(d, slot)
                copy.wait_recv()
                copy.wait_send()

    def wide_y(half, x):
        return cat([jnp.broadcast_to(half[i : i + 1], (Y, Z)) for i in range(x)])

    def wide_z(half, x):
        return cat([jnp.broadcast_to(half[:, i : i + 1], (Y, Z)) for i in range(x)])

    def operate(v, level, slot):
        w = levs[level]
        step = 1 << level
        x = X >> level
        start(v, slot)
        acc = w[DG] * v
        acc = acc - w[YM] * roll(v, step, 0) - w[YP] * roll(v, -step, 0)
        acc = acc - w[ZM] * roll(v, step, 1) - w[ZP] * roll(v, -step, 1)
        if x > 1:
            none = jnp.zeros((Y, Z), jnp.float32)
            acc = acc - w[XM] * cat([none, v[:-Y]]) - w[XP] * cat([v[Y:], none])
        finish(slot)
        in_y = jnp.where(rows_of(x) < Y // 2, wide_y(ry[slot, 0], x), wide_y(ry[slot, 1], x))
        in_z = jnp.where(lanes_of(x) < Z // 2, wide_z(rz[slot, 0], x), wide_z(rz[slot, 1], x))
        acc = acc - w[YB] * in_y - w[ZB] * in_z
        low = w[XM, :Y] * rx[slot, 0]
        high = w[XP, (x - 1) * Y :] * rx[slot, 1]
        if x == 1:
            return acc - low - high
        parts = [acc[:Y] - low] + ([acc[Y:-Y]] if x > 2 else []) + [acc[-Y:] - high]
        return cat(parts)

    def pair_x(v):
        x = v.shape[0] // Y
        return cat([v[2 * i * Y : (2 * i + 1) * Y] + v[(2 * i + 1) * Y : (2 * i + 2) * Y] for i in range(x // 2)])

    def pick_x(v, odd):
        x = v.shape[0] // Y
        return cat([v[(2 * i + odd) * Y : (2 * i + odd + 1) * Y] for i in range(x // 2)])

    def bit(v, level, axis):
        at = rows_of(v.shape[0] // Y) if axis == 0 else lanes_of(v.shape[0] // Y)
        return lax.rem(at, 2 << level) < (1 << level)

    def pair(v, level, axis):
        step = 1 << level
        return v + jnp.where(bit(v, level, axis), roll(v, -step, axis), roll(v, step, axis))

    def pick(v, level, axis, odd):
        step = 1 << level
        low = bit(v, level, axis)
        if odd:
            return jnp.where(low, roll(v, -step, axis), v)
        return jnp.where(low, v, roll(v, step, axis))

    def restrict(v, level):
        return pair(pair(pair_x(v), level, 0), level, 1)

    def prolong(v):
        x = v.shape[0] // Y
        return cat([v[(i // 2) * Y : (i // 2 + 1) * Y] for i in range(2 * x)])

    def put_level(level, ws, reaction):
        xm, xp, ym, yp, zm, zp = ws
        w = levs[level]
        step = 1 << level
        x = X >> level
        rows, lanes = rows_of(x), lanes_of(x)
        diagonal = reaction + xm + xp + ym + yp + zm + zp
        zero = jnp.zeros_like(xm)
        w[DG] = diagonal
        w[INV] = 1.0 / diagonal
        w[XM] = xm
        w[XP] = xp
        w[YM] = jnp.where(rows < step, zero, ym)
        w[YP] = jnp.where(rows >= Y - step, zero, yp)
        w[ZM] = jnp.where(lanes < step, zero, zm)
        w[ZP] = jnp.where(lanes >= Z - step, zero, zp)
        w[YB] = jnp.where(rows < step, ym, jnp.where(rows >= Y - step, yp, zero))
        w[ZB] = jnp.where(lanes < step, zm, jnp.where(lanes >= Z - step, zp, zero))

    turn = [0]

    def apply(v, level):
        slot = turn[0] % ROUND
        turn[0] += 1
        return operate(v, level, slot)

    def vcycle(r, level):
        w = levs[level]
        u = w[INV] * r * (1.0 / MID)
        total = u
        r = r - apply(u, level)
        u = RHO1 * RHO0 * u + 2.0 * RHO1 / HALF * w[INV] * r
        total = total + u
        r = r - apply(u, level)
        if level == LEVELS - 1:
            u = RHO2 * RHO1 * u + 2.0 * RHO2 / HALF * w[INV] * r
            return total + u
        e = prolong(vcycle(restrict(r, level), level + 1))
        total = total + e
        r = r - apply(e, level)
        u = w[INV] * r * (1.0 / MID)
        total = total + u
        r = r - apply(u, level)
        u = RHO1 * RHO0 * u + 2.0 * RHO1 / HALF * w[INV] * r
        return total + u

    def gather(ref, part, count, me, device, which):
        for j in range(count):
            @pl.when(me != j)
            def _():
                pltpu.make_async_remote_copy(
                    src_ref=ref.at[part, me],
                    dst_ref=ref.at[part, me],
                    send_sem=red_ssem.at[which, part],
                    recv_sem=red_rsem.at[which, part],
                    device_id=device(j),
                    device_id_type=MESH,
                ).start()
        if count > 1:
            others = ref.at[part, pl.ds(0, count - 1)]
            pltpu.make_async_copy(others, others, red_rsem.at[which, part]).wait()
            pltpu.make_async_copy(others, others, red_ssem.at[which, part]).wait()

    def in_plane(j):
        return (ix, j // nz, j % nz)

    def in_column(j):
        return (j, iy, iz)

    my_plane = iy * nz + iz

    def reduce_plane(ref, part, value, which):
        ref[part, my_plane] = value
        gather(ref, part, planes, my_plane, in_plane, which)
        return jnp.sum(ref[part], axis=0)

    def reduce_column(ref, part, value, which):
        ref[part, ix] = value
        gather(ref, part, nx, ix, in_column, which)
        return jnp.sum(ref[part], axis=0)

    def total_of(v):
        return jnp.sum(jnp.sum(v, axis=0, keepdims=True), axis=1, keepdims=True)

    def lane_of(row, i):
        return jnp.sum(jnp.where(lane_1 == i, row, 0.0), axis=1, keepdims=True)

    it = it_ref[...].reshape(X * Y, Z)
    reaction = rea_ref[...].reshape(X * Y, Z)
    start(it, KEPT)
    finish(KEPT)
    rows, lanes = rows_of(X), lanes_of(X)
    last_row, last_lane = rows == Y - 1, lanes == Z - 1
    n_xm = cat([rx[KEPT, 0], it[:-Y]])
    n_xp = cat([it[Y:], rx[KEPT, 1]])
    n_ym = jnp.where(rows == 0, wide_y(ry[KEPT, 0], X), roll(it, 1, 0))
    n_yp = jnp.where(last_row, wide_y(ry[KEPT, 1], X), roll(it, -1, 0))
    n_zm = jnp.where(lanes == 0, wide_z(rz[KEPT, 0], X), roll(it, 1, 1))
    n_zp = jnp.where(last_lane, wide_z(rz[KEPT, 1], X), roll(it, -1, 1))
    ws = []
    r = src_ref[...].reshape(X * Y, Z) - reaction * it
    for sign, n in ((-1, n_xm), (1, n_xp), (-1, n_ym), (1, n_yp), (-1, n_zm), (1, n_zp)):
        g = n - it
        square = g * g
        root = jnp.sqrt(1.0 + square)
        ws.append((1.0 + 2.0 * square) / root)
        r = r + g * root
    rem_ref[...] = r.reshape(X, Y, Z)
    put_level(0, ws, reaction)
    for level in range(LEVELS - 1):
        xm, xp, ym, yp, zm, zp = ws
        ws = (
            pair(pair(pick_x(xm, 0), level, 0), level, 1),
            pair(pair(pick_x(xp, 1), level, 0), level, 1),
            pair(pick(pair_x(ym), level, 0, 0), level, 1),
            pair(pick(pair_x(yp), level, 0, 1), level, 1),
            pick(pair(pair_x(zm), level, 0), level, 1, 0),
            pick(pair(pair_x(zp), level, 0), level, 1, 1),
        )
        reaction = restrict(reaction, level)
        put_level(level + 1, ws, reaction)
    for ref in (p_ref, q_ref, phx, phy, phz, dhx, dhy, dhz):
        ref[...] = jnp.zeros_like(ref)
    dir_ref[...] = jnp.zeros_like(dir_ref)

    def body(it_idx, carry):
        rz_old, pq_old = carry
        part = lax.rem(it_idx, 2)
        r = rem_ref[...].reshape(X * Y, Z)
        turn[0] = 0
        z = vcycle(r, 0)
        z_slot = turn[0] % ROUND
        az = apply(z, 0)
        q_old = q_ref[...]
        sums = jnp.where(
            lane_1 == 0,
            total_of(rem_ref[...].reshape(X * Y, Z) * z),
            jnp.where(lane_1 == 1, total_of(z * az), total_of(z * q_old)),
        )
        row = reduce_plane(dot_pl, part, sums, 0)
        row = reduce_column(dot_x, part, row, 1)
        rz_new, zaz, zq = lane_of(row, 0), lane_of(row, 1), lane_of(row, 2)
        beta = rz_new / rz_old
        pq = zaz + 2.0 * beta * zq + beta * beta * pq_old
        a = rz_new / pq
        p = z + beta * p_ref[...]
        q = az + beta * q_old
        p_ref[...] = p
        q_ref[...] = q
        dir_ref[...] = dir_ref[...] + (a * p).reshape(X, Y, Z)
        rem_ref[...] = rem_ref[...] - (a * q).reshape(X, Y, Z)
        for got, ph, dh in ((rx, phx, dhx), (ry, phy, dhy), (rz, phz, dhz)):
            for side in range(2):
                edge = got[z_slot, side] + beta * ph[side]
                ph[side] = edge
                dh[side] = dh[side] + a * edge
        return rz_new, pq

    one = jnp.ones((1, 1), jnp.float32)
    lax.fori_loop(0, ITERS, body, (one, jnp.zeros((1, 1), jnp.float32)))

    it = it_ref[...].reshape(X * Y, Z)
    step_dir = dir_ref[...].reshape(X * Y, Z)

    def energy(g):
        square = 1.0 + g * g
        return (square * jnp.sqrt(square) - 1.0) * (1.0 / 3.0)

    ends_y = jnp.where(jnp.logical_and(last_row, iy == ny - 1), 1.0, 0.0)
    ends_z = jnp.where(jnp.logical_and(last_lane, iz == nz - 1), 1.0, 0.0)
    ends_x = jnp.where(ix == nx - 1, 1.0, 0.0)
    across = lax.broadcasted_iota(jnp.int32, (X, Z), 0) == lax.broadcasted_iota(jnp.int32, (X, Z), 1)
    trial_rows = []
    for k in range(TRIALS):
        s = jnp.exp2(-jnp.full((1, Z), tp_ref[k], jnp.int32).astype(jnp.float32))
        v = it + s * step_dir
        low_x = cat([rx[KEPT, 0] + s * dhx[0], v[:-Y]])
        low_y = jnp.where(rows == 0, wide_y(ry[KEPT, 0] + s * dhy[0], X), roll(v, 1, 0))
        low_z = jnp.where(lanes == 0, wide_z(rz[KEPT, 0] + s * dhz[0], X), roll(v, 1, 1))
        at_end = energy(v)
        e = energy(v - low_x) + energy(v - low_y) + energy(v - low_z)
        e = e + at_end * (ends_y + ends_z)
        e = cat([e[:-Y], e[-Y:] + ends_x * at_end[-Y:]]) if X > 1 else e + ends_x * at_end
        e = e + 0.5 * rea_ref[...].reshape(X * Y, Z) * v * v - src_ref[...].reshape(X * Y, Z) * v
        by_layer = jnp.sum(jnp.sum(e.reshape(X, Y, Z), axis=1), axis=1, keepdims=True)
        trial_rows.append(jnp.sum(jnp.where(across, by_layer, 0.0), axis=0, keepdims=True))
    layers = reduce_plane(en_pl, 0, jnp.concatenate(trial_rows, axis=0), 2)
    layers = layers / (Y * ny * Z * nz)
    le_ref[...] = layers[:, :X]
    overall = reduce_column(en_x, 0, layers, 3)
    overall = jnp.sum(overall, axis=1, keepdims=True) / (X * nx)
    en_ref[...] = jnp.broadcast_to(overall, (TRIALS, Z))


def on_device(counts, iterate, source, reaction, trial_powers):
    X, Y, Z = iterate.shape
    nx, ny, nz = counts
    f32 = jnp.float32
    slots = ROUND + 1
    vm = pltpu.VMEM
    scratch = [vm((slots, 2, rows, Z), f32) for rows in (Y, Y, X, X, Y, Y)]
    scratch += [pltpu.SemaphoreType.DMA((slots, 6))] * 2
    scratch += [vm((10, (X >> level) * Y, Z), f32) for level in range(LEVELS)]
    scratch += [vm((X * Y, Z), f32)] * 2
    scratch += [vm((2, rows, Z), f32) for rows in (Y, X, Y)] * 2
    scratch += [
        vm((2, ny * nz, 1, Z), f32), vm((2, nx, 1, Z), f32),
        vm((1, ny * nz, TRIALS, Z), f32), vm((1, nx, TRIALS, Z), f32),
        pltpu.SemaphoreType.DMA((4, 2)), pltpu.SemaphoreType.DMA((4, 2)),
    ]
    whole = pl.BlockSpec(memory_space=pltpu.VMEM)
    out = pl.pallas_call(
        functools.partial(kernel, (X, Y, Z), counts),
        out_shape=[
            jax.ShapeDtypeStruct((X, Y, Z), f32),
            jax.ShapeDtypeStruct((X, Y, Z), f32),
            jax.ShapeDtypeStruct((TRIALS, X), f32),
            jax.ShapeDtypeStruct((TRIALS, Z), f32),
        ],
        in_specs=[pl.BlockSpec(memory_space=pltpu.SMEM), whole, whole, whole],
        out_specs=[whole] * 4,
        scratch_shapes=scratch,
        compiler_params=pltpu.CompilerParams(has_side_effects=True, vmem_limit_bytes=48 * 1024 * 1024),
        name="newton_step",
    )(trial_powers, iterate, source, reaction)
    return out[0], out[1], out[2], out[3][:, 0]


def solution(mesh):
    counts = tuple(mesh.shape[axis] for axis in ("gx", "gy", "gz"))
    grid = P("gx", "gy", "gz")
    return jax.shard_map(
        functools.partial(on_device, counts),
        mesh=mesh,
        in_specs=(grid, grid, grid, P()),
        out_specs=(grid, grid, P(None, "gx"), P()),
        check_vma=False,
    )
```

time: 1850 us -> 221 us (0.12)
  starting transfers between devices: 977 us -> 0 us
  waiting for transfers between devices: 400 us -> 0 us
  blocking collectives: 339 us -> 0 us
  Pallas kernels: 0 us -> 214 us
  local copies, waits for them, and re-layouts: 50.2 us -> 5.63 us
  other arithmetic: 42.2 us -> 0 us
  between operations: 23.4 us -> 0.65 us
    ppermute x372 -> x0, starting transfers between devices: 977 us -> none  [the longest x186 736 us: padded_2(): before = lax.ppermute(last, axis, up)]
    ppermute x372 -> x0, waiting for transfers between devices: 400 us -> none  [the longest x186 230 us: padded_2(): after = lax.ppermute(first, axis, down)]
    psum x9 -> x0, blocking collectives: 339 us -> none  [the longest x4 178 us: precond_dot(): return lax.psum(jnp.sum(left * right), ('gx', 'gy', 'gz'))]
    pallas_call x0 -> x1, Pallas kernels: none -> 214 us  [on_device(): pl.pallas_call(functools.partial(kernel, (X, Y, Z), counts), out_shape=[j...]
    slice x167 -> x1, local copies, waits for them, and re-layouts: 22.2 us -> 0.63 us  [on_device(): return (out[0], out[1], out[2], out[3][:, 0])]
  transfers between devices with their start and end apart: 372 -> 0, of which waited for: 217 -> 0; matrix products, arithmetic and copies ran while one was open for 1% -> 0% of each run, Pallas kernels for 0% -> 0%
where the time goes in v1:
time: 221 us; the launch traced here: 220 us
  Pallas kernels  214 us (97%)
  local copies, waits for them, and re-layouts  5.63 us (3%)
    pallas_call x1, Pallas kernels, on_device(): pl.pallas_call(functools.partial(kernel, (X, Y, Z), counts), out_shape=[j...  214 us
    unnamed x11, local copies, waits for them, and re-layouts  5 us

profile of v1, /device:TPU:0, one launch (start us, length us, event | category | flops | bytes accessed | tf_op | source)
XLA Modules:
  0.0 220.3 jit_solution(15238309877620704371)
XLA Ops:
  0.6 0.0 copy-start
  0.6 0.8 copy-done
  1.5 0.0 copy-start.1
  1.5 0.8 copy-done.1
  2.3 0.0 copy-start.2
  2.3 0.8 copy-done.2
  3.2 0.0 copy-start.3
  3.2 0.7 copy-done.3
  3.8 214.0 %newton_step.1 = (f32[8,16,128]{2,1,0:T(8,128)S(1)}, f32[8,16,128]{2,1,0:T(8,128)S(1)}, f32[4,8]{1,0:T(4,128)S(1)}, f32[4,128]{1,0:T(4,128)S(1)}) custom-call(s32[4]{0:T(128)S(1)} %copy-done.3, f32[8,16,128]{2,1,0:T(8,128)S(1)} %copy-done, f32[8,16,128]{2,1,0:T(8,128)S(1)} %copy-done.1, f32[8,16,128]{2,1,0:T(8,128)S(1)} %copy-done.2), custom_call_target="tpu_custom_call" | custom-call | tf_op jit(solution)/shard_map/newton_step/pallas_call | solution.py:386
  217.8 0.6 slice_reduce_fusion
  218.4 0.6 copy.11
  219.1 0.6 copy.12
  219.7 0.6 copy.13
Async XLA Ops:
  0.6 0.8 copy-start
  1.5 0.8 copy-start.1
  2.3 0.8 copy-start.2
  3.2 0.7 copy-start.3

commit v2 on v1

--- a/solution.py
+++ b/solution.py
@@ -22,15 +22,123 @@
 MESH = pl.DeviceIdType.MESH
 
 
+class Grid:
+    def __init__(self, Y, Z):
+        self.Y, self.Z = Y, Z
+
+    def rows_of(self, x):
+        return lax.rem(lax.broadcasted_iota(jnp.int32, (x * self.Y, self.Z), 0), self.Y)
+
+    def lanes_of(self, x):
+        return lax.broadcasted_iota(jnp.int32, (x * self.Y, self.Z), 1)
+
+    def pair_x(self, v):
+        Y = self.Y
+        x = v.shape[0] // Y
+        return cat([v[2 * i * Y : (2 * i + 1) * Y] + v[(2 * i + 1) * Y : (2 * i + 2) * Y] for i in range(x // 2)])
+
+    def pick_x(self, v, odd):
+        Y = self.Y
+        x = v.shape[0] // Y
+        return cat([v[(2 * i + odd) * Y : (2 * i + odd + 1) * Y] for i in range(x // 2)])
+
+    def bit(self, v, level, axis):
+        at = self.rows_of(v.shape[0] // self.Y) if axis == 0 else self.lanes_of(v.shape[0] // self.Y)
+        return lax.rem(at, 2 << level) < (1 << level)
+
+    def pair(self, v, level, axis):
+        step = 1 << level
+        return v + jnp.where(self.bit(v, level, axis), roll(v, -step, axis), roll(v, step, axis))
+
+    def pick(self, v, level, axis, odd):
+        step = 1 << level
+        low = self.bit(v, level, axis)
+        if odd:
+            return jnp.where(low, roll(v, -step, axis), v)
+        return jnp.where(low, v, roll(v, step, axis))
+
+    def restrict(self, v, level):
+        return self.pair(self.pair(self.pair_x(v), level, 0), level, 1)
+
+    def prolong(self, v):
+        Y = self.Y
+        x = v.shape[0] // Y
+        return cat([v[(i // 2) * Y : (i // 2 + 1) * Y] for i in range(2 * x)])
+
+    def coarsen(self, ws, reaction, level):
+        xm, xp, ym, yp, zm, zp = ws
+        pair, pick = self.pair, self.pick
+        ws = (
+            pair(pair(self.pick_x(xm, 0), level, 0), level, 1),
+            pair(pair(self.pick_x(xp, 1), level, 0), level, 1),
+            pair(pick(self.pair_x(ym), level, 0, 0), level, 1),
+            pair(pick(self.pair_x(yp), level, 0, 1), level, 1),
+            pick(pair(self.pair_x(zm), level, 0), level, 1, 0),
+            pick(pair(self.pair_x(zp), level, 0), level, 1, 1),
+        )
+        return ws, self.restrict(reaction, level)
+
+    def put(self, w, level, ws, reaction):
+        Y, Z = self.Y, self.Z
+        xm, xp, ym, yp, zm, zp = ws
+        step = 1 << level
+        x = xm.shape[0] // Y
+        rows, lanes = self.rows_of(x), self.lanes_of(x)
+        diagonal = reaction + xm + xp + ym + yp + zm + zp
+        zero = jnp.zeros_like(xm)
+        w[DG] = diagonal
+        w[INV] = 1.0 / diagonal
+        w[XM] = xm
+        w[XP] = xp
+        w[YM] = jnp.where(rows < step, zero, ym)
+        w[YP] = jnp.where(rows >= Y - step, zero, yp)
+        w[ZM] = jnp.where(lanes < step, zero, zm)
+        w[ZP] = jnp.where(lanes >= Z - step, zero, zp)
+        if w.shape[0] > YB:
+            w[YB] = jnp.where(rows < step, ym, jnp.where(rows >= Y - step, yp, zero))
+            w[ZB] = jnp.where(lanes < step, zm, jnp.where(lanes >= Z - step, zp, zero))
+
+    def inner(self, w, v, level):
+        step = 1 << level
+        acc = w[DG] * v
+        acc = acc - w[YM] * roll(v, step, 0) - w[YP] * roll(v, -step, 0)
+        acc = acc - w[ZM] * roll(v, step, 1) - w[ZP] * roll(v, -step, 1)
+        Y = self.Y
+        if v.shape[0] > Y:
+            none = jnp.zeros((Y, self.Z), jnp.float32)
+            acc = acc - w[XM] * cat([none, v[:-Y]]) - w[XP] * cat([v[Y:], none])
+        return acc
+
+
+def cat(parts):
+    return parts[0] if len(parts) == 1 else jnp.concatenate(parts, axis=0)
+
+
+def roll(v, shift, axis):
+    return pltpu.roll(v, shift % v.shape[axis], axis)
+
+
+def dot(a, b):
+    return lax.dot_general(
+        a, b, (((1,), (0,)), ((), ())), precision=lax.Precision.HIGHEST, preferred_element_type=jnp.float32
+    )
+
+
 def kernel(
     sizes, counts, tp_ref, it_ref, src_ref, rea_ref, dir_ref, rem_ref, le_ref, en_ref,
-    sx, rx, sy, ry, sz, rz, ssem, rsem, lev0, lev1, lev2, lev3, p_ref, q_ref,
+    sx, rx, sy, ry, sz, rz, ssem, rsem, lev0, lev1, glev2, glev3, p_ref, q_ref,
     phx, phy, phz, dhx, dhy, dhz, dot_pl, dot_x, en_pl, en_x, red_ssem, red_rsem,
+    picked, gat_pl, gat_x, set_pl, set_x, glob,
 ):
     X, Y, Z = sizes
     nx, ny, nz = counts
     planes = ny * nz
-    levs = (lev0, lev1, lev2, lev3)
+    levs = (lev0, lev1)
+    L = len(levs)
+    x_own, y_own, z_own = X >> L, Y >> L, Z >> L
+    GY, GZ = ny * y_own, nz * z_own
+    here, world = Grid(Y, Z), Grid(GY, GZ)
+    rows_of, lanes_of = here.rows_of, here.lanes_of
     ix, iy, iz = lax.axis_index("gx"), lax.axis_index("gy"), lax.axis_index("gz")
     has = (ix > 0, ix < nx - 1, iy > 0, iy < ny - 1, iz > 0, iz < nz - 1)
     devs = (
@@ -41,18 +149,6 @@
     recv = (rx, rx, ry, ry, rz, rz)
     lane_y = lax.broadcasted_iota(jnp.int32, (Y, Z), 1)
     lane_1 = lax.broadcasted_iota(jnp.int32, (1, Z), 1)
-
-    def rows_of(x):
-        return lax.rem(lax.broadcasted_iota(jnp.int32, (x * Y, Z), 0), Y)
-
-    def lanes_of(x):
-        return lax.broadcasted_iota(jnp.int32, (x * Y, Z), 1)
-
-    def cat(parts):
-        return parts[0] if len(parts) == 1 else jnp.concatenate(parts, axis=0)
-
-    def roll(v, shift, axis):
-        return pltpu.roll(v, shift % v.shape[axis], axis)
 
     for d in range(6):
         @pl.when(jnp.logical_not(has[d]))
@@ -120,76 +216,24 @@
     def wide_z(half, x):
         return cat([jnp.broadcast_to(half[:, i : i + 1], (Y, Z)) for i in range(x)])
 
+    def beyond(w, acc, in_x0, in_x1, in_y, in_z):
+        x = acc.shape[0] // Y
+        acc = acc - w[YB] * in_y - w[ZB] * in_z
+        low = w[XM, :Y] * in_x0
+        high = w[XP, (x - 1) * Y :] * in_x1
+        if x == 1:
+            return acc - low - high
+        return cat([acc[:Y] - low] + ([acc[Y:-Y]] if x > 2 else []) + [acc[-Y:] - high])
+
     def operate(v, level, slot):
         w = levs[level]
-        step = 1 << level
         x = X >> level
         start(v, slot)
-        acc = w[DG] * v
-        acc = acc - w[YM] * roll(v, step, 0) - w[YP] * roll(v, -step, 0)
-        acc = acc - w[ZM] * roll(v, step, 1) - w[ZP] * roll(v, -step, 1)
-        if x > 1:
-            none = jnp.zeros((Y, Z), jnp.float32)
-            acc = acc - w[XM] * cat([none, v[:-Y]]) - w[XP] * cat([v[Y:], none])
+        acc = here.inner(w, v, level)
         finish(slot)
         in_y = jnp.where(rows_of(x) < Y // 2, wide_y(ry[slot, 0], x), wide_y(ry[slot, 1], x))
         in_z = jnp.where(lanes_of(x) < Z // 2, wide_z(rz[slot, 0], x), wide_z(rz[slot, 1], x))
-        acc = acc - w[YB] * in_y - w[ZB] * in_z
-        low = w[XM, :Y] * rx[slot, 0]
-        high = w[XP, (x - 1) * Y :] * rx[slot, 1]
-        if x == 1:
-            return acc - low - high
-        parts = [acc[:Y] - low] + ([acc[Y:-Y]] if x > 2 else []) + [acc[-Y:] - high]
-        return cat(parts)
-
-    def pair_x(v):
-        x = v.shape[0] // Y
-        return cat([v[2 * i * Y : (2 * i + 1) * Y] + v[(2 * i + 1) * Y : (2 * i + 2) * Y] for i in range(x // 2)])
-
-    def pick_x(v, odd):
-        x = v.shape[0] // Y
-        return cat([v[(2 * i + odd) * Y : (2 * i + odd + 1) * Y] for i in range(x // 2)])
-
-    def bit(v, level, axis):
-        at = rows_of(v.shape[0] // Y) if axis == 0 else lanes_of(v.shape[0] // Y)
-        return lax.rem(at, 2 << level) < (1 << level)
-
-    def pair(v, level, axis):
-        step = 1 << level
-        return v + jnp.where(bit(v, level, axis), roll(v, -step, axis), roll(v, step, axis))
-
-    def pick(v, level, axis, odd):
-        step = 1 << level
-        low = bit(v, level, axis)
-        if odd:
-            return jnp.where(low, roll(v, -step, axis), v)
-        return jnp.where(low, v, roll(v, step, axis))
-
-    def restrict(v, level):
-        return pair(pair(pair_x(v), level, 0), level, 1)
-
-    def prolong(v):
-        x = v.shape[0] // Y
-        return cat([v[(i // 2) * Y : (i // 2 + 1) * Y] for i in range(2 * x)])
-
-    def put_level(level, ws, reaction):
-        xm, xp, ym, yp, zm, zp = ws
-        w = levs[level]
-        step = 1 << level
-        x = X >> level
-        rows, lanes = rows_of(x), lanes_of(x)
-        diagonal = reaction + xm + xp + ym + yp + zm + zp
-        zero = jnp.zeros_like(xm)
-        w[DG] = diagonal
-        w[INV] = 1.0 / diagonal
-        w[XM] = xm
-        w[XP] = xp
-        w[YM] = jnp.where(rows < step, zero, ym)
-        w[YP] = jnp.where(rows >= Y - step, zero, yp)
-        w[ZM] = jnp.where(lanes < step, zero, zm)
-        w[ZP] = jnp.where(lanes >= Z - step, zero, zp)
-        w[YB] = jnp.where(rows < step, ym, jnp.where(rows >= Y - step, yp, zero))
-        w[ZB] = jnp.where(lanes < step, zm, jnp.where(lanes >= Z - step, zp, zero))
+        return beyond(w, acc, rx[slot, 0], rx[slot, 1], in_y, in_z)
 
     turn = [0]
 
@@ -198,7 +242,7 @@
         turn[0] += 1
         return operate(v, level, slot)
 
-    def vcycle(r, level):
+    def vcycle(r, level, part):
         w = levs[level]
         u = w[INV] * r * (1.0 / MID)
         total = u
@@ -206,17 +250,98 @@
         u = RHO1 * RHO0 * u + 2.0 * RHO1 / HALF * w[INV] * r
         total = total + u
         r = r - apply(u, level)
-        if level == LEVELS - 1:
-            u = RHO2 * RHO1 * u + 2.0 * RHO2 / HALF * w[INV] * r
-            return total + u
-        e = prolong(vcycle(restrict(r, level), level + 1))
+        coarse = here.restrict(r, level)
+        if level + 1 < L:
+            e = here.prolong(vcycle(coarse, level + 1, part))
+            r = r - apply(e, level)
+        else:
+            everywhere = collect(coarse, 1, part, gat_pl, gat_x, 4)
+            e, ends = spread(world_cycle(everywhere[0], level + 1))
+            r = r - beyond(w, here.inner(w, e, level), *ends)
         total = total + e
-        r = r - apply(e, level)
         u = w[INV] * r * (1.0 / MID)
         total = total + u
         r = r - apply(u, level)
         u = RHO1 * RHO0 * u + 2.0 * RHO1 / HALF * w[INV] * r
         return total + u
+
+    def world_cycle(r, level):
+        w = (glev2, glev3)[level - L]
+
+        def apply(v):
+            return world.inner(w, v, level - L)
+
+        u = w[INV] * r * (1.0 / MID)
+        total = u
+        r = r - apply(u)
+        u = RHO1 * RHO0 * u + 2.0 * RHO1 / HALF * w[INV] * r
+        total = total + u
+        r = r - apply(u)
+        if level == LEVELS - 1:
+            u = RHO2 * RHO1 * u + 2.0 * RHO2 / HALF * w[INV] * r
+            return total + u
+        e = world.prolong(world_cycle(world.restrict(r, level - L), level + 1))
+        total = total + e
+        r = r - apply(e)
+        u = w[INV] * r * (1.0 / MID)
+        total = total + u
+        r = r - apply(u)
+        u = RHO1 * RHO0 * u + 2.0 * RHO1 / HALF * w[INV] * r
+        return total + u
+
+    def hot(shape, wanted):
+        at = lax.broadcasted_iota(jnp.int32, shape, 0)
+        return jnp.where(at == wanted, 1.0, 0.0)
+
+    def collect(v, fields, part, pl_ref, x_ref, which):
+        count = fields * x_own * y_own
+        picked[: fields * x_own * Y] = v
+        own = picked[pl.ds(0, count, stride=1 << L), :]
+        lane = lax.broadcasted_iota(jnp.int32, (Z, GZ), 1) - iz * z_own
+        inside = jnp.logical_and(lane >= 0, lane < z_own)
+        put = hot((Z, GZ), jnp.where(inside, lane * (1 << L), -1))
+        pl_ref[part, my_plane] = dot(own, put)
+        gather(pl_ref, part, planes, my_plane, in_plane, which)
+        for j in range(ny):
+            rows = pl_ref[part, j * nz]
+            for k in range(1, nz):
+                rows = rows + pl_ref[part, j * nz + k]
+            for i in range(fields * x_own):
+                x_ref[part, ix, i * GY + j * y_own : i * GY + (j + 1) * y_own] = rows[i * y_own : (i + 1) * y_own]
+        gather(x_ref, part, nx, ix, in_column, which + 1)
+        return [
+            cat([x_ref[part, d, f * x_own * GY : (f + 1) * x_own * GY] for d in range(nx)]) for f in range(fields)
+        ]
+
+    def spread(v):
+        lane = lax.broadcasted_iota(jnp.int32, (GZ, Z), 1)
+        inside = hot((GZ, Z), iz * z_own + lane // (1 << L))
+        outside = hot((GZ, Z), jnp.where(lane < Z // 2, iz * z_own - 1, iz * z_own + z_own))
+        glob[0, GY : GY + nx * x_own * GY] = dot(v, inside)
+        glob[1, GY : GY + nx * x_own * GY] = dot(v, outside)
+        rows = rows_of(1)
+
+        def layer(which, a):
+            base = (ix * x_own + 1 + a) * GY + iy * y_own
+            out = jnp.broadcast_to(glob[which, pl.ds(base, 1), :], (Y, Z))
+            for j in range(1, y_own):
+                row = jnp.broadcast_to(glob[which, pl.ds(base + j, 1), :], (Y, Z))
+                out = jnp.where(rows < j << L, out, row)
+            return out
+
+        def rims(a):
+            base = (ix * x_own + 1 + a) * GY + iy * y_own
+            low = glob[0, pl.ds(base - 1, 1), :] * has_low
+            high = glob[0, pl.ds(base + y_own, 1), :] * has_high
+            return jnp.where(rows < Y // 2, jnp.broadcast_to(low, (Y, Z)), jnp.broadcast_to(high, (Y, Z)))
+
+        has_low = jnp.where(iy > 0, 1.0, 0.0)
+        has_high = jnp.where(iy < ny - 1, 1.0, 0.0)
+        own = range(x_own)
+        e = here.prolong(cat([layer(0, a) for a in own]))
+        in_y = here.prolong(cat([rims(a) for a in own]))
+        in_z = here.prolong(cat([layer(1, a) for a in own]))
+        return e, (layer(0, -1), layer(0, x_own), in_y, in_z)
 
     def gather(ref, part, count, me, device, which):
         for j in range(count):
@@ -280,19 +405,15 @@
         ws.append((1.0 + 2.0 * square) / root)
         r = r + g * root
     rem_ref[...] = r.reshape(X, Y, Z)
-    put_level(0, ws, reaction)
-    for level in range(LEVELS - 1):
-        xm, xp, ym, yp, zm, zp = ws
-        ws = (
-            pair(pair(pick_x(xm, 0), level, 0), level, 1),
-            pair(pair(pick_x(xp, 1), level, 0), level, 1),
-            pair(pick(pair_x(ym), level, 0, 0), level, 1),
-            pair(pick(pair_x(yp), level, 0, 1), level, 1),
-            pick(pair(pair_x(zm), level, 0), level, 1, 0),
-            pick(pair(pair_x(zp), level, 0), level, 1, 1),
-        )
-        reaction = restrict(reaction, level)
-        put_level(level + 1, ws, reaction)
+    here.put(levs[0], 0, ws, reaction)
+    for level in range(L):
+        ws, reaction = here.coarsen(ws, reaction, level)
+        if level + 1 < L:
+            here.put(levs[level + 1], level + 1, ws, reaction)
+    glob[...] = jnp.zeros_like(glob)
+    *ws, reaction = collect(cat(list(ws) + [reaction]), 7, 0, set_pl, set_x, 6)
+    world.put(glev2, 0, ws, reaction)
+    world.put(glev3, 1, *world.coarsen(ws, reaction, 0))
     for ref in (p_ref, q_ref, phx, phy, phz, dhx, dhy, dhz):
         ref[...] = jnp.zeros_like(ref)
     dir_ref[...] = jnp.zeros_like(dir_ref)
@@ -302,7 +423,7 @@
         part = lax.rem(it_idx, 2)
         r = rem_ref[...].reshape(X * Y, Z)
         turn[0] = 0
-        z = vcycle(r, 0)
+        z = vcycle(r, 0, part)
         z_slot = turn[0] % ROUND
         az = apply(z, 0)
         q_old = q_ref[...]
@@ -374,13 +495,20 @@
     vm = pltpu.VMEM
     scratch = [vm((slots, 2, rows, Z), f32) for rows in (Y, Y, X, X, Y, Y)]
     scratch += [pltpu.SemaphoreType.DMA((slots, 6))] * 2
-    scratch += [vm((10, (X >> level) * Y, Z), f32) for level in range(LEVELS)]
+    x_own, y_own = X // 4, Y // 4
+    GX, GY, GZ = nx * x_own, ny * y_own, nz * Z // 4
+    scratch += [vm((10, (X >> level) * Y, Z), f32) for level in range(2)]
+    scratch += [vm((8, (GX >> level) * GY, GZ), f32) for level in range(2)]
     scratch += [vm((X * Y, Z), f32)] * 2
     scratch += [vm((2, rows, Z), f32) for rows in (Y, X, Y)] * 2
     scratch += [
         vm((2, ny * nz, 1, Z), f32), vm((2, nx, 1, Z), f32),
         vm((1, ny * nz, TRIALS, Z), f32), vm((1, nx, TRIALS, Z), f32),
-        pltpu.SemaphoreType.DMA((4, 2)), pltpu.SemaphoreType.DMA((4, 2)),
+        pltpu.SemaphoreType.DMA((8, 2)), pltpu.SemaphoreType.DMA((8, 2)),
+        vm((7 * x_own * Y, Z), f32),
+        vm((2, ny * nz, x_own * y_own, GZ), f32), vm((2, nx, x_own * GY, GZ), f32),
+        vm((1, ny * nz, 7 * x_own * y_own, GZ), f32), vm((1, nx, 7 * x_own * GY, GZ), f32),
+        vm((2, (GX + 2) * GY, Z), f32),
     ]
     whole = pl.BlockSpec(memory_space=pltpu.VMEM)
     out = pl.pallas_call(

time: 221 us -> 186 us (0.84)
  Pallas kernels: 214 us -> 180 us
    pallas_call x1, Pallas kernels: 214 us -> 180 us  [on_device(): pl.pallas_call(functools.partial(kernel, (X, Y, Z), counts), out_shape=[j...]
where the time goes in v2:
time: 186 us
  Pallas kernels  180 us (97%)
  local copies, waits for them, and re-layouts  5.63 us (3%)
    pallas_call x1, Pallas kernels, on_device(): pl.pallas_call(functools.partial(kernel, (X, Y, Z), counts), out_shape=[j...  180 us
    unnamed x11, local copies, waits for them, and re-layouts  5 us

profile of v2, /device:TPU:0, one launch (start us, length us, event | category | flops | bytes accessed | tf_op | source)
XLA Modules:
  0.0 186.2 jit_solution(5261582931257137681)
XLA Ops:
  0.6 0.0 copy-start
  0.6 0.8 copy-done
  1.5 0.0 copy-start.1
  1.5 0.8 copy-done.1
  2.3 0.0 copy-start.2
  2.3 0.8 copy-done.2
  3.2 0.0 copy-start.3
  3.2 0.7 copy-done.3
  3.8 179.9 %newton_step.1 = (f32[8,16,128]{2,1,0:T(8,128)S(1)}, f32[8,16,128]{2,1,0:T(8,128)S(1)}, f32[4,8]{1,0:T(4,128)S(1)}, f32[4,128]{1,0:T(4,128)S(1)}) custom-call(s32[4]{0:T(128)S(1)} %copy-done.3, f32[8,16,128]{2,1,0:T(8,128)S(1)} %copy-done, f32[8,16,128]{2,1,0:T(8,128)S(1)} %copy-done.1, f32[8,16,128]{2,1,0:T(8,128)S(1)} %copy-done.2), custom_call_target="tpu_custom_call" | custom-call | tf_op jit(solution)/shard_map/newton_step/pallas_call | solution.py:514
  183.7 0.6 slice_reduce_fusion
  184.4 0.6 copy.11
  185.0 0.6 copy.12
  185.6 0.6 copy.13
Async XLA Ops:
  0.6 0.8 copy-start
  1.5 0.8 copy-start.1
  2.3 0.8 copy-start.2
  3.2 0.7 copy-start.3

commit v3 on v2

--- a/solution.py
+++ b/solution.py
@@ -127,7 +127,7 @@
 def kernel(
     sizes, counts, tp_ref, it_ref, src_ref, rea_ref, dir_ref, rem_ref, le_ref, en_ref,
     sx, rx, sy, ry, sz, rz, ssem, rsem, lev0, lev1, glev2, glev3, p_ref, q_ref,
-    phx, phy, phz, dhx, dhy, dhz, dot_pl, dot_x, en_pl, en_x, red_ssem, red_rsem,
+    phx, phy, phz, dhx, dhy, dhz, dot_all, en_pl, en_x, red_ssem, red_rsem,
     picked, gat_pl, gat_x, set_pl, set_x, glob,
 ):
     X, Y, Z = sizes
@@ -366,7 +366,11 @@
     def in_column(j):
         return (j, iy, iz)
 
+    def in_grid(j):
+        return (j // planes, j // nz % ny, j % nz)
+
     my_plane = iy * nz + iz
+    me = ix * planes + my_plane
 
     def reduce_plane(ref, part, value, which):
         ref[part, my_plane] = value
@@ -432,8 +436,9 @@
             total_of(rem_ref[...].reshape(X * Y, Z) * z),
             jnp.where(lane_1 == 1, total_of(z * az), total_of(z * q_old)),
         )
-        row = reduce_plane(dot_pl, part, sums, 0)
-        row = reduce_column(dot_x, part, row, 1)
+        dot_all[part, me] = sums
+        gather(dot_all, part, nx * planes, me, in_grid, 0)
+        row = jnp.sum(dot_all[part], axis=0)
         rz_new, zaz, zq = lane_of(row, 0), lane_of(row, 1), lane_of(row, 2)
         beta = rz_new / rz_old
         pq = zaz + 2.0 * beta * zq + beta * beta * pq_old
@@ -502,7 +507,7 @@
     scratch += [vm((X * Y, Z), f32)] * 2
     scratch += [vm((2, rows, Z), f32) for rows in (Y, X, Y)] * 2
     scratch += [
-        vm((2, ny * nz, 1, Z), f32), vm((2, nx, 1, Z), f32),
+        vm((2, nx * ny * nz, 1, Z), f32),
         vm((1, ny * nz, TRIALS, Z), f32), vm((1, nx, TRIALS, Z), f32),
         pltpu.SemaphoreType.DMA((8, 2)), pltpu.SemaphoreType.DMA((8, 2)),
         vm((7 * x_own * Y, Z), f32),

time: 186 us -> 178 us (0.957)
  Pallas kernels: 180 us -> 172 us
    pallas_call x1, Pallas kernels: 180 us -> 172 us  [on_device(): pl.pallas_call(functools.partial(kernel, (X, Y, Z), counts), out_shape=[j...]
where the time goes in v3:
time: 178 us
  Pallas kernels  172 us (97%)
  local copies, waits for them, and re-layouts  5.63 us (3%)
    pallas_call x1, Pallas kernels, on_device(): pl.pallas_call(functools.partial(kernel, (X, Y, Z), counts), out_shape=[j...  172 us
    unnamed x11, local copies, waits for them, and re-layouts  5 us

profile of v3, /device:TPU:0, one launch (start us, length us, event | category | flops | bytes accessed | tf_op | source)
XLA Modules:
  0.0 178.0 jit_solution(11453904724913037189)
XLA Ops:
  0.6 0.0 copy-start
  0.6 0.8 copy-done
  1.5 0.0 copy-start.1
  1.5 0.8 copy-done.1
  2.3 0.0 copy-start.2
  2.3 0.8 copy-done.2
  3.2 0.0 copy-start.3
  3.2 0.7 copy-done.3
  3.8 171.7 %newton_step.1 = (f32[8,16,128]{2,1,0:T(8,128)S(1)}, f32[8,16,128]{2,1,0:T(8,128)S(1)}, f32[4,8]{1,0:T(4,128)S(1)}, f32[4,128]{1,0:T(4,128)S(1)}) custom-call(s32[4]{0:T(128)S(1)} %copy-done.3, f32[8,16,128]{2,1,0:T(8,128)S(1)} %copy-done, f32[8,16,128]{2,1,0:T(8,128)S(1)} %copy-done.1, f32[8,16,128]{2,1,0:T(8,128)S(1)} %copy-done.2), custom_call_target="tpu_custom_call" | custom-call | tf_op jit(solution)/shard_map/newton_step/pallas_call | solution.py:519
  175.6 0.6 slice_reduce_fusion
  176.2 0.6 copy.11
  176.8 0.6 copy.12
  177.4 0.6 copy.13
Async XLA Ops:
  0.6 0.8 copy-start
  1.5 0.8 copy-start.1
  2.3 0.8 copy-start.2
  3.2 0.7 copy-start.3

commit v4 on v3

--- a/solution.py
+++ b/solution.py
@@ -127,7 +127,7 @@
 def kernel(
     sizes, counts, tp_ref, it_ref, src_ref, rea_ref, dir_ref, rem_ref, le_ref, en_ref,
     sx, rx, sy, ry, sz, rz, ssem, rsem, lev0, lev1, glev2, glev3, p_ref, q_ref,
-    phx, phy, phz, dhx, dhy, dhz, dot_all, en_pl, en_x, red_ssem, red_rsem,
+    phx, phy, phz, dhx, dhy, dhz, dot_all, en_all, red_ssem, red_rsem,
     picked, gat_pl, gat_x, set_pl, set_x, glob,
 ):
     X, Y, Z = sizes
@@ -484,10 +484,12 @@
         e = e + 0.5 * rea_ref[...].reshape(X * Y, Z) * v * v - src_ref[...].reshape(X * Y, Z) * v
         by_layer = jnp.sum(jnp.sum(e.reshape(X, Y, Z), axis=1), axis=1, keepdims=True)
         trial_rows.append(jnp.sum(jnp.where(across, by_layer, 0.0), axis=0, keepdims=True))
-    layers = reduce_plane(en_pl, 0, jnp.concatenate(trial_rows, axis=0), 2)
+    en_all[0, me] = jnp.concatenate(trial_rows, axis=0)
+    gather(en_all, 0, nx * planes, me, in_grid, 2)
+    layers = jnp.sum(en_all[0, pl.ds(ix * planes, planes)], axis=0)
     layers = layers / (Y * ny * Z * nz)
     le_ref[...] = layers[:, :X]
-    overall = reduce_column(en_x, 0, layers, 3)
+    overall = jnp.sum(en_all[0], axis=0) / (Y * ny * Z * nz)
     overall = jnp.sum(overall, axis=1, keepdims=True) / (X * nx)
     en_ref[...] = jnp.broadcast_to(overall, (TRIALS, Z))
 
@@ -508,7 +510,7 @@
     scratch += [vm((2, rows, Z), f32) for rows in (Y, X, Y)] * 2
     scratch += [
         vm((2, nx * ny * nz, 1, Z), f32),
-        vm((1, ny * nz, TRIALS, Z), f32), vm((1, nx, TRIALS, Z), f32),
+        vm((1, nx * ny * nz, TRIALS, Z), f32),
         pltpu.SemaphoreType.DMA((8, 2)), pltpu.SemaphoreType.DMA((8, 2)),
         vm((7 * x_own * Y, Z), f32),
         vm((2, ny * nz, x_own * y_own, GZ), f32), vm((2, nx, x_own * GY, GZ), f32),

time: 178 us -> 176 us (0.989)
  Pallas kernels: 172 us -> 170 us
    pallas_call x1, Pallas kernels: 172 us -> 170 us  [on_device(): pl.pallas_call(functools.partial(kernel, (X, Y, Z), counts), out_shape=[j...]
where the time goes in v4:
time: 176 us
  Pallas kernels  170 us (97%)
  local copies, waits for them, and re-layouts  5.63 us (3%)
    pallas_call x1, Pallas kernels, on_device(): pl.pallas_call(functools.partial(kernel, (X, Y, Z), counts), out_shape=[j...  170 us
    unnamed x11, local copies, waits for them, and re-layouts  5 us

profile of v4, /device:TPU:0, one launch (start us, length us, event | category | flops | bytes accessed | tf_op | source)
XLA Modules:
  0.0 175.9 jit_solution(5050277093254199309)
XLA Ops:
  0.6 0.0 copy-start
  0.6 0.8 copy-done
  1.5 0.0 copy-start.1
  1.5 0.8 copy-done.1
  2.3 0.0 copy-start.2
  2.3 0.8 copy-done.2
  3.2 0.0 copy-start.3
  3.2 0.7 copy-done.3
  3.8 169.6 %newton_step.1 = (f32[8,16,128]{2,1,0:T(8,128)S(1)}, f32[8,16,128]{2,1,0:T(8,128)S(1)}, f32[4,8]{1,0:T(4,128)S(1)}, f32[4,128]{1,0:T(4,128)S(1)}) custom-call(s32[4]{0:T(128)S(1)} %copy-done.3, f32[8,16,128]{2,1,0:T(8,128)S(1)} %copy-done, f32[8,16,128]{2,1,0:T(8,128)S(1)} %copy-done.1, f32[8,16,128]{2,1,0:T(8,128)S(1)} %copy-done.2), custom_call_target="tpu_custom_call" | custom-call | tf_op jit(solution)/shard_map/newton_step/pallas_call | solution.py:521
  173.4 0.6 slice_reduce_fusion
  174.1 0.6 copy.11
  174.7 0.6 copy.12
  175.3 0.6 copy.13
Async XLA Ops:
  0.6 0.8 copy-start
  1.5 0.8 copy-start.1
  2.3 0.8 copy-start.2
  3.2 0.7 copy-start.3
